TPU v7x, 32 devices: a whole 2x2x4 slice. The times are simulated.
32 devices in a mesh: dof: 16 (over z, x, core), mode: 2 (over y).
Axes of the slice: x: 2, y: 2, z: 4, core: 2. Of those that a mesh axis runs over, the one named last changes fastest.
Arguments:
- stiffness_tiles: bfloat16 [512, 10, 128, 128], P('dof'), may hold values from -0.15625 to 0.15625
- tile_cols: int32 [512, 10], P('dof'), may hold values from 0 to 47, as said below
- send_rows: int32 [32, 8], P('dof'), may hold values from 0 to 31, as said below
- block: bfloat16 [65536, 128], P('dof', 'mode'), may hold values from -51 to 51
- lower_bound: float32 [1], replicated, may hold values from -1.2 to -0.6
- upper_bound: float32 [1], replicated, may hold values from 0.4 to 0.9
Outputs:
- basis: bfloat16 [65536, 128], P('dof', 'mode')
- ritz: float32 [128, 128], replicated
Inputs may be any that keep to these rules, and one draw needn't show every extreme that they name: `tile_cols`: entry 0 of every tile row is that row's own local index; entry 1 is a code of the lower neighbour's upward list and entry 2 a code of the upper neighbour's downward list. A code below 32 is a tile row of the same partition; 32 + s is slot s of the lower neighbour's upward list; 40 + s is slot s of the upper neighbour's downward list. `send_rows`: rows 2 p and 2 p + 1 hold distinct local tile rows of partition p: its downward and upward send lists.
All inputs are finite; a program needn't handle non-finite values.
Results may differ from a plain program's by a relative error of at most 0.0086.
Values may be sent and summed in bfloat16 or wider, within the bound.
A program may use at most 64 MiB of HBM per device.

v0:
```python
import jax
import jax.numpy as jnp
from jax import lax
from jax.sharding import PartitionSpec as P


def shifted(block, axis, distance):
    devices = range(lax.axis_size(axis))
    route = [(i - distance, i) for i in devices if i - distance in devices]
    return lax.ppermute(block, axis, route)


def reduce_factor(gram_matrix, projected):
    factor = jnp.linalg.cholesky(gram_matrix)
    identity = jnp.eye(gram_matrix.shape[0], dtype=jnp.float32)
    inverse = jax.scipy.linalg.solve_triangular(factor, identity, lower=True)
    ritz_matrix = jnp.dot(
        jnp.dot(inverse, projected, precision=lax.Precision.HIGHEST),
        inverse.T,
        precision=lax.Precision.HIGHEST,
    )
    return (ritz_matrix, inverse.T.astype(jnp.bfloat16))


def shards(stiffness_tiles, tile_cols, send_rows, block, lower_bound, upper_bound):
    row_count, mode_cols = block.shape
    row_tiles = stiffness_tiles.shape[0]
    tile_size = stiffness_tiles.shape[2]
    dof_total = row_count * lax.axis_size("dof")
    center = (upper_bound[0] + lower_bound[0]) * 0.5
    half_width = (upper_bound[0] - lower_bound[0]) * 0.5

    def apply_stiffness(field):
        field_cube = field.reshape(row_tiles, tile_size, mode_cols)
        upward = field_cube[send_rows[1]]
        downward = field_cube[send_rows[0]]
        from_lower = shifted(upward, "dof", 1)
        from_upper = shifted(downward, "dof", -1)
        extended = jnp.concatenate([field_cube, from_lower, from_upper], axis=0)
        picked = extended[tile_cols]
        result = jnp.einsum(
            "rkij,rkjm->rim", stiffness_tiles, picked, preferred_element_type=jnp.float32
        )
        return result.reshape(row_count, mode_cols)

    previous = block
    current = ((apply_stiffness(block) - center * block.astype(jnp.float32)) / half_width).astype(
        jnp.bfloat16
    )
    following = (
        2.0 * (apply_stiffness(current) - center * current.astype(jnp.float32)) / half_width
        - previous.astype(jnp.float32)
    ).astype(jnp.bfloat16)
    previous, current = (current, following)
    image_block = apply_stiffness(current).astype(jnp.bfloat16)
    whole_block = lax.all_gather(current, "mode", axis=1, tiled=True)
    gram_part = jnp.dot(whole_block.T, current, preferred_element_type=jnp.float32)
    proj_part = jnp.dot(whole_block.T, image_block, preferred_element_type=jnp.float32)
    my_index = lax.axis_index("mode")
    gram_cols, proj_cols = lax.psum((gram_part, proj_part), "dof")
    gram_matrix, projected = (
        lax.all_gather(gram_cols, "mode", axis=1, tiled=True),
        lax.all_gather(proj_cols, "mode", axis=1, tiled=True),
    )
    ritz_matrix, right_factor = reduce_factor(gram_matrix / dof_total, projected / dof_total)
    own_factor = lax.dynamic_slice_in_dim(right_factor, my_index * mode_cols, mode_cols, 1)
    basis_out = jnp.dot(whole_block, own_factor, preferred_element_type=jnp.float32).astype(
        jnp.bfloat16
    )
    return (basis_out, ritz_matrix)


def solution(mesh):
    placed = (
        P("dof", None, None, None),
        P("dof", None),
        P("dof", None),
        P("dof", "mode"),
        P(),
        P(),
    )
    return jax.shard_map(
        shards, mesh=mesh, in_specs=placed, out_specs=(P("dof", "mode"), P()), check_vma=False
    )
```

profile of v0, /device:TPU:0, one launch (start us, length us, event | category | flops | bytes accessed | tf_op | source)
XLA Modules:
  0.0 246.6 jit_solution(9108452360754528071)
XLA Ops:
  7.2 0.8 fusion.18
  8.0 1.2 copy_bitcast_fusion.2
  9.2 0.6 gather_fusion
  9.7 2.4 collective-permute-start
  12.7 1.3 collective-permute-start.1
  14.0 0.7 compare_select_fusion
  16.3 1.8 collective-permute-done.1
  18.2 13.3 %gather_fusion.2 = bf16[320,128,64]{1,2,0:T(8,128)(2,1)} fusion(bf16[48,128,64]{1,2,0:T(8,128)(2,1)S(1)} %pad_maximum_fusion, s32[1024]{0:T(1024)S(1)} %pad_clamp_fusion), kind=kCustom, calls=%fused_computation.2 | custom fusion | bytes 10487040 | tf_op jit(solution)/shard_map/gather | solution.py:40
  31.5 9.2 %convolution_bitcast_fusion.2 = f32[32,8,8,128]{3,2,1,0:T(8,128)S(1)} fusion(bf16[32,10,128,64]{2,3,1,0:T(8,128)(2,1)} %bitcast.86, bf16[32,10,128,128]{3,2,1,0:T(8,128)(2,1)} %param.6), kind=kOutput, calls=%fused_computation.12 | convolution fusion | flops 671088640 | bytes 16777216 | tf_op jit(solution)/shard_map/rkij,rkjm->rim/dot_general | solution.py:41
  41.1 0.6 gather_fusion.3
  42.3 5.5 %collective-permute-start.2 = (bf16[8,128,64]{1,2,0:T(8,128)(2,1)S(1)}, bf16[8,128,64]{1,2,0:T(8,128)(2,1)S(1)}, u32[]{:S(2)}, u32[]{:S(2)}) collective-permute-start(bf16[8,128,64]{1,2,0:T(8,128)(2,1)S(1)} %gather_fusion.3), channel_id=1, source_target_pairs={{0,2},{2,4},{4,6},{6,8},{8,10},{10,12},{12,14},{14,16},{16,18},{18... | collective-permute-start | bytes 393224 | tf_op jit(solution)/shard_map/ppermute | solution.py:10
  47.7 1.5 collective-permute-start.3
  49.2 1.8 collective-permute-done.3
  51.1 13.3 %gather_fusion.5 = bf16[320,128,64]{1,2,0:T(8,128)(2,1)} fusion(bf16[48,128,64]{1,2,0:T(8,128)(2,1)S(1)} %pad_maximum_fusion.1, s32[1024]{0:T(1024)S(1)} %pad_clamp_fusion), kind=kCustom, calls=%fused_computation.5 | custom fusion | bytes 10487040 | tf_op jit(solution)/shard_map/gather | solution.py:40
  64.4 9.2 %convolution_bitcast_fusion.1 = f32[32,8,8,128]{3,2,1,0:T(8,128)S(1)} fusion(bf16[32,10,128,64]{2,3,1,0:T(8,128)(2,1)} %bitcast.87, bf16[32,10,128,128]{3,2,1,0:T(8,128)(2,1)} %param.6), kind=kOutput, calls=%fused_computation.11 | convolution fusion | flops 671088640 | bytes 16777216 | tf_op jit(solution)/shard_map/rkij,rkjm->rim/dot_general | solution.py:41
  74.1 0.6 gather_fusion.6
  75.2 5.8 %collective-permute-start.4 = (bf16[8,128,64]{1,2,0:T(8,128)(2,1)S(1)}, bf16[8,128,64]{1,2,0:T(8,128)(2,1)S(1)}, u32[]{:S(2)}, u32[]{:S(2)}) collective-permute-start(bf16[8,128,64]{1,2,0:T(8,128)(2,1)S(1)} %gather_fusion.6), channel_id=1, source_target_pairs={{0,2},{2,4},{4,6},{6,8},{8,10},{10,12},{12,14},{14,16},{16,18},{18... | collective-permute-start | bytes 393224 | tf_op jit(solution)/shard_map/ppermute | solution.py:10
  81.0 1.3 collective-permute-start.5
  82.6 1.6 collective-permute-done.5
  84.4 13.3 %gather_fusion.8 = bf16[320,128,64]{1,2,0:T(8,128)(2,1)} fusion(bf16[48,128,64]{1,2,0:T(8,128)(2,1)S(1)} %pad_maximum_fusion.2, s32[1024]{0:T(1024)S(1)} %pad_clamp_fusion), kind=kCustom, calls=%fused_computation.8 | custom fusion | bytes 10487040 | tf_op jit(solution)/shard_map/gather | solution.py:40
  97.7 9.3 %fusion.1 = bf16[32,8,8,128]{3,2,1,0:T(8,128)(2,1)S(1)} fusion(bf16[32,10,128,64]{2,3,1,0:T(8,128)(2,1)} %bitcast.85, bf16[32,10,128,128]{3,2,1,0:T(8,128)(2,1)} %param.6), kind=kOutput, calls=%fused_computation.16 | convolution fusion | flops 671350784 | bytes 16252928 | tf_op jit(solution)/shard_map/rkij,rkjm->rim/dot_general | solution.py:41
  107.0 2.3 fusion.22
  109.3 2.3 fusion.8
  111.7 91.5 %all-reduce.3.cloned.1.call-done = (f32[128,64]{0,1:T(8,128)}, f32[128,64]{0,1:T(8,128)}) async-done(((f32[128,64]{0,1:T(8,128)}, f32[128,64]{0,1:T(8,128)}), (f32[128,64]{0,1:T(8,128)}, f32[128,64]{0,1:T(8,128)})) %all-reduce.3.cloned.1.call-update) | async-done | bytes 65552 | tf_op jit(solution)/shard_map/psum | solution.py:60
  203.2 5.0 %all_gather.10 = f32[128,128]{0,1:T(8,128)S(1)} all-gather(f32[128,64]{0,1:T(8,128)} %get-tuple-element.2), channel_id=1, replica_groups=mesh['dof'=16,'mode'=2] {'mode'}, dimensions={1}, use_global_device_ids=true | all-gather | bytes 98304 | tf_op jit(solution)/shard_map/all_gather | solution.py:62
  208.4 11.7 %cholesky.17 = f32[128,128]{1,0:T(8,128)S(1)} custom-call(f32[128,128]{1,0:T(8,128)S(1)} %fusion.14), custom_call_target="Cholesky" | custom-call | tf_op jit(solution)/shard_map/jit(cholesky)/cholesky | solution.py:14
  220.1 0.6 compare_reduce_fusion
  220.8 0.7 fusion.11
  221.4 9.8 %custom-call.7 = f32[1,128,128]{1,2,0:T(8,128)S(1)} custom-call(f32[1,128,128]{2,1,0:T(8,128)S(1)} %fusion.11), custom_call_target="InvertDiagBlocksLowerTriangular" | custom-call | tf_op jit(solution)/shard_map/jit(_solve_triangular)/triangular_solve | solution.py:16
  231.5 4.8 %all_gather.11 = f32[128,128]{0,1:T(8,128)S(1)} all-gather(f32[128,64]{0,1:T(8,128)} %get-tuple-element.3), channel_id=1, replica_groups=mesh['dof'=16,'mode'=2] {'mode'}, dimensions={1}, use_global_device_ids=true | all-gather | bytes 98304 | tf_op jit(solution)/shard_map/all_gather | solution.py:63
  236.5 0.9 fusion.23
  237.4 2.3 convolution_convert_fusion
  (35 shorter events, 3.9 us)
Async XLA Ops:
  7.2 99.8 %all-gather.2.cloned.1.call-start = ((), (), s32[]{:S(2)}) async-start(), calls=%async_computation | async-start | bytes 1572864 | tf_op jit(solution)/shard_map/all_gather | solution.py:56
  9.7 6.5 %collective-permute-start = (bf16[8,128,64]{1,2,0:T(8,128)(2,1)S(1)}, bf16[8,128,64]{1,2,0:T(8,128)(2,1)S(1)}, u32[]{:S(2)}, u32[]{:S(2)}) collective-permute-start(bf16[8,128,64]{1,2,0:T(8,128)(2,1)S(1)} %gather_fusion), channel_id=1, source_target_pairs={{0,2},{2,4},{4,6},{6,8},{8,10},{10,12},{12,14},{14,16},{16,18},{18... | collective-permute-start | bytes 393224 | tf_op jit(solution)/shard_map/ppermute | solution.py:10
  12.7 5.3 %collective-permute-start.1 = (bf16[8,128,64]{1,2,0:T(8,128)(2,1)S(1)}, bf16[8,128,64]{1,2,0:T(8,128)(2,1)S(1)}, u32[]{:S(2)}, u32[]{:S(2)}) collective-permute-start(bf16[8,128,64]{1,2,0:T(8,128)(2,1)S(1)} %gather_fusion.1), channel_id=1, source_target_pairs={{2,0},{4,2},{6,4},{8,6},{10,8},{12,10},{14,12},{16,14},{18,16},{20... | collective-permute-start | bytes 393224 | tf_op jit(solution)/shard_map/ppermute | solution.py:10
  31.5 9.3 %copy-start.2 = (bf16[4096,64]{0,1:T(8,128)(2,1)S(1)}, bf16[4096,64]{0,1:T(8,128)(2,1)}, u32[]{:S(2)}) copy-start(bf16[4096,64]{0,1:T(8,128)(2,1)} %param.9) | copy-start | bytes 1572868
  42.3 6.9 %collective-permute-start.2 = (bf16[8,128,64]{1,2,0:T(8,128)(2,1)S(1)}, bf16[8,128,64]{1,2,0:T(8,128)(2,1)S(1)}, u32[]{:S(2)}, u32[]{:S(2)}) collective-permute-start(bf16[8,128,64]{1,2,0:T(8,128)(2,1)S(1)} %gather_fusion.3), channel_id=1, source_target_pairs={{0,2},{2,4},{4,6},{6,8},{8,10},{10,12},{12,14},{14,16},{16,18},{18... | collective-permute-start | bytes 393224 | tf_op jit(solution)/shard_map/ppermute | solution.py:10
  47.7 3.2 %collective-permute-start.3 = (bf16[8,128,64]{1,2,0:T(8,128)(2,1)S(1)}, bf16[8,128,64]{1,2,0:T(8,128)(2,1)S(1)}, u32[]{:S(2)}, u32[]{:S(2)}) collective-permute-start(bf16[8,128,64]{1,2,0:T(8,128)(2,1)S(1)} %gather_fusion.4), channel_id=1, source_target_pairs={{2,0},{4,2},{6,4},{8,6},{10,8},{12,10},{14,12},{16,14},{18,16},{20... | collective-permute-start | bytes 393224 | tf_op jit(solution)/shard_map/ppermute | solution.py:10
  73.9 8.4 %copy-start = (bf16[4096,64]{0,1:T(8,128)(2,1)}, bf16[4096,64]{0,1:T(8,128)(2,1)S(1)}, u32[]{:S(2)}) copy-start(bf16[4096,64]{0,1:T(8,128)(2,1)S(1)} %fusion.5) | copy-start | bytes 1572868
  75.2 7.4 %collective-permute-start.4 = (bf16[8,128,64]{1,2,0:T(8,128)(2,1)S(1)}, bf16[8,128,64]{1,2,0:T(8,128)(2,1)S(1)}, u32[]{:S(2)}, u32[]{:S(2)}) collective-permute-start(bf16[8,128,64]{1,2,0:T(8,128)(2,1)S(1)} %gather_fusion.6), channel_id=1, source_target_pairs={{0,2},{2,4},{4,6},{6,8},{8,10},{10,12},{12,14},{14,16},{16,18},{18... | collective-permute-start | bytes 393224 | tf_op jit(solution)/shard_map/ppermute | solution.py:10
  81.0 3.2 %collective-permute-start.5 = (bf16[8,128,64]{1,2,0:T(8,128)(2,1)S(1)}, bf16[8,128,64]{1,2,0:T(8,128)(2,1)S(1)}, u32[]{:S(2)}, u32[]{:S(2)}) collective-permute-start(bf16[8,128,64]{1,2,0:T(8,128)(2,1)S(1)} %gather_fusion.7), channel_id=1, source_target_pairs={{2,0},{4,2},{6,4},{8,6},{10,8},{12,10},{14,12},{16,14},{18,16},{20... | collective-permute-start | bytes 393224 | tf_op jit(solution)/shard_map/ppermute | solution.py:10
  82.3 120.9 %all-reduce.3.cloned.1.call-start = ((), (), s32[]{:S(2)}) async-start(), calls=%async_computation.1 | async-start | bytes 131072 | tf_op jit(solution)/shard_map/psum | solution.py:60
  97.7 9.3 %copy-start.1 = (bf16[4096,64]{0,1:T(8,128)(2,1)S(1)}, bf16[4096,64]{0,1:T(8,128)(2,1)}, u32[]{:S(2)}) copy-start(bf16[4096,64]{0,1:T(8,128)(2,1)} %copy-done) | copy-start | bytes 1572868
Sparse Core Ops, SparseCore 0:
  82.5 24.2 all-gather.1
  111.8 91.3 all-reduce.2
where the time goes:
time: 248 us; the launch traced here: 247 us
  waiting for transfers between devices  96.8 us (39%)
  local copies, waits for them, and re-layouts  45.2 us (18%)
  matrix products  36.1 us (15%)
  other arithmetic  25.1 us (10%)
  starting transfers between devices  18 us (7%)
  between operations  15.7 us (6%)
  blocking collectives  9.84 us (4%)
    psum x1, waiting for transfers between devices, shards(): gram_cols, proj_cols = lax.psum((gram_part, proj_part), 'dof')  91.5 us
    gather x3, local copies, waits for them, and re-layouts, apply_stiffness(): picked = extended[tile_cols]  40 us
    dot_general x3, matrix products, apply_stiffness(): jnp.einsum('rkij,rkjm->rim', stiffness_tiles, picked, preferred_element_t...  27.7 us
    ppermute x6, starting transfers between devices, shifted(): return lax.ppermute(block, axis, route)  17.7 us
    another operation x3, other arithmetic, reduce_factor(): factor = jnp.linalg.cholesky(gram_matrix)  12.4 us
    another operation x2, other arithmetic, reduce_factor(): inverse = jax.scipy.linalg.solve_triangular(factor, identity, lower=True)  10.5 us
    ppermute x6, waiting for transfers between devices, shifted(): return lax.ppermute(block, axis, route)  5.19 us
    all_gather x1, blocking collectives, shards(): lax.all_gather(gram_cols, 'mode', axis=1, tiled=True)  5.04 us
  transfers between devices with their start and end apart: 8, of which 4 were waited for; matrix products, arithmetic and copies ran while one was open for 10% of the time, Pallas kernels for 0%

commit v1 on v0

v1 whole, which is shorter than its diff:
```python
import functools

import jax
import jax.numpy as jnp
from jax import lax
from jax.experimental import pallas as pl
from jax.experimental.pallas import tpu as pltpu
from jax.sharding import PartitionSpec as P

MESH = pl.DeviceIdType.MESH
NT = (((1,), (1,)), ((), ()))
NN = (((1,), (0,)), ((), ()))
TN = (((0,), (0,)), ((), ()))
EXACT = lax.Precision.HIGHEST


def kernel(
    parts, cols, rows, low_ref, high_ref, x_ref, a_hbm, basis_ref, ritz_ref,
    a_ref, level0, level1, level2, plain, image, other, sends, ar_send, ar_recv,
    work, inv_ref, inv_t,
    a_sem, halo_send, halo_recv, mode_send, mode_recv, ar_ssem, ar_rsem,
):
    tiles, nnz, size = a_ref.shape[0], a_ref.shape[1], a_ref.shape[2]
    modes = x_ref.shape[0]
    width = 2 * modes
    slots = rows.shape[1]
    stages = ar_send.shape[0] - 1
    chunks = mode_send.shape[0]
    part_rows = tiles // chunks
    p = lax.axis_index("dof")
    my = lax.axis_index("mode")
    has_low = p > 0
    has_up = p < parts - 1

    loads = []
    a_parts = a_sem.shape[0]
    for i in range(a_parts):
        span = pl.ds(i * (tiles // a_parts), tiles // a_parts)
        loads.append(pltpu.make_async_copy(a_hbm.at[span], a_ref.at[span], a_sem.at[i]))
        loads[-1].start()

    def flipped(bit):
        return p + bit * (1 - 2 * ((p // bit) % 2))

    barrier = pltpu.get_barrier_semaphore()
    for s in range(stages):
        pl.semaphore_signal(barrier, inc=1, device_id=(flipped(1 << s), my), device_id_type=MESH)
    pl.semaphore_signal(barrier, inc=1, device_id=(p, 1 - my), device_id_type=MESH)

    @pl.when(has_low)
    def _():
        pl.semaphore_signal(barrier, inc=1, device_id=(p - 1, my), device_id_type=MESH)

    @pl.when(has_up)
    def _():
        pl.semaphore_signal(barrier, inc=1, device_id=(p + 1, my), device_id_type=MESH)

    for t in range(tiles):
        tile = x_ref[:, t * size : (t + 1) * size]
        level0[t] = tile
        plain[t] = tile

    @pl.when(p == 0)
    def _():
        for level in (level0, level1, level2):
            level[tiles : tiles + slots] = jnp.zeros((slots, modes, size), jnp.bfloat16)

    @pl.when(p == parts - 1)
    def _():
        for level in (level0, level1, level2):
            level[tiles + slots :] = jnp.zeros((slots, modes, size), jnp.bfloat16)

    for s in range(slots):
        sends[0, s] = plain[rows[1, s]]
        sends[0, slots + s] = plain[rows[0, s]]

    pl.semaphore_wait(
        barrier, stages + 1 + has_low.astype(jnp.int32) + has_up.astype(jnp.int32)
    )

    def halo(index, level):
        up = pltpu.make_async_remote_copy(
            src_ref=sends.at[index, pl.ds(0, slots)],
            dst_ref=level.at[pl.ds(tiles, slots)],
            send_sem=halo_send.at[index, 0],
            recv_sem=halo_recv.at[index, 0],
            device_id=(lax.rem(p + 1, parts), my),
            device_id_type=MESH,
        )
        down = pltpu.make_async_remote_copy(
            src_ref=sends.at[index, pl.ds(slots, slots)],
            dst_ref=level.at[pl.ds(tiles + slots, slots)],
            send_sem=halo_send.at[index, 1],
            recv_sem=halo_recv.at[index, 1],
            device_id=(lax.rem(p + parts - 1, parts), my),
            device_id_type=MESH,
        )
        return up, down

    def start_halo(index, level):
        up, down = halo(index, level)
        pl.when(has_up)(up.start)
        pl.when(has_low)(down.start)

    def wait_halo(index, level):
        up, down = halo(index, level)
        pl.when(has_low)(up.wait_recv)
        pl.when(has_up)(down.wait_recv)
        pl.when(has_up)(up.wait_send)
        pl.when(has_low)(down.wait_send)

    start_halo(0, level0)

    center = (high_ref[0] + low_ref[0]) * 0.5
    half_width = (high_ref[0] - low_ref[0]) * 0.5
    scale = jnp.ones((1, size), jnp.float32) / jnp.full((1, size), half_width, jnp.float32)

    def product(level, t):
        field = jnp.concatenate([level[cols[k, t]] for k in range(nnz)], axis=1)
        stored = jnp.concatenate([a_ref[t, k] for k in range(nnz)], axis=1)
        return lax.dot_general(field, stored, NT, preferred_element_type=jnp.float32)

    def first(t):
        own = level0[t].astype(jnp.float32)
        return ((product(level0, t) - center * own) * scale).astype(jnp.bfloat16)

    def second(t):
        own = level1[t].astype(jnp.float32)
        before = level0[t].astype(jnp.float32)
        return (2.0 * (product(level1, t) - center * own) * scale - before).astype(jnp.bfloat16)

    def send_tiles(index, make):
        @pl.loop(0, slots // 2)
        def _(i):
            made = []
            for u in range(2):
                s = i * 2 + u
                made.append((s, make(rows[1, s])))
                made.append((slots + s, make(rows[0, s])))
            for s, value in made:
                sends[index, s] = value

    def all_tiles(make, target, begin, count, group=4):
        @pl.loop(0, count // group)
        def _(i):
            made = [make(begin + i * group + u) for u in range(group)]
            for u in range(group):
                target[begin + i * group + u] = made[u]

    for load in loads:
        load.wait()
    wait_halo(0, level0)
    send_tiles(1, first)
    start_halo(1, level1)
    all_tiles(first, level1, 0, tiles)
    wait_halo(1, level1)
    send_tiles(2, second)
    start_halo(2, level2)

    def exchange(c):
        span = pl.ds(c * part_rows, part_rows)
        return pltpu.make_async_remote_copy(
            src_ref=level2.at[span],
            dst_ref=other.at[span],
            send_sem=mode_send.at[c],
            recv_sem=mode_recv.at[c],
            device_id=(p, 1 - my),
            device_id_type=MESH,
        )

    for c in range(chunks):
        all_tiles(second, level2, c * part_rows, part_rows)
        exchange(c).start()
    wait_halo(2, level2)
    all_tiles(lambda t: product(level2, t).astype(jnp.bfloat16), image, 0, tiles)

    total = jnp.zeros((width, width), jnp.float32)
    for c in range(chunks):
        exchange(c).wait_recv()

        def accumulate(i, acc):
            left, right = [], []
            for u in range(4):
                t = c * part_rows + i * 4 + u
                left.append(jnp.concatenate([level2[t], image[t]], axis=0))
                right.append(jnp.concatenate([level2[t], other[t]], axis=0))
            return acc + lax.dot_general(
                jnp.concatenate(left, axis=1), jnp.concatenate(right, axis=1), NT,
                preferred_element_type=jnp.float32,
            )

        total = lax.fori_loop(0, part_rows // 4, accumulate, total)
    total = jnp.where(my == 1, pltpu.roll(total, modes, 1), total)

    for s in range(stages + 1):
        partner = (flipped(1 << s), my) if s < stages else (p, 1 - my)
        ar_send[s] = total
        copy = pltpu.make_async_remote_copy(
            src_ref=ar_send.at[s],
            dst_ref=ar_recv.at[s],
            send_sem=ar_ssem.at[s],
            recv_sem=ar_rsem.at[s],
            device_id=partner,
            device_id_type=MESH,
        )
        copy.start()
        copy.wait()
        if s < stages:
            total = total + ar_recv[s]
    theirs = ar_recv[stages]
    count = parts * tiles * size
    lower = jnp.where(my == 0, total, theirs) / count
    upper = jnp.where(my == 0, theirs, total) / count
    gram = jnp.concatenate([lower[:modes], upper[:modes]], axis=0)
    projected_t = jnp.concatenate([lower[modes:], upper[modes:]], axis=0)

    step = 16
    row_id = lax.broadcasted_iota(jnp.int32, (width, width), 0)
    col_id = lax.broadcasted_iota(jnp.int32, (width, width), 1)
    work[:, :width] = gram
    work[:, width:] = (row_id == col_id).astype(jnp.float32)
    small = lax.broadcasted_iota(jnp.int32, (step, 1), 0)
    lanes = lax.broadcasted_iota(jnp.int32, (step, width), 1)

    @pl.loop(0, width // step)
    def _(b):
        begin = pl.multiple_of(b * step, step)
        panel = work[pl.ds(begin, step), :]
        near = panel[:, :width]
        columns = [
            jnp.sum(jnp.where(lanes == begin + s, near, 0.0), axis=1, keepdims=True)
            for s in range(step)
        ]
        pivots = jnp.zeros((step, 1), jnp.float32)
        for q in range(step):
            pivot = columns[q][q : q + 1, :]
            pivots = jnp.where(small == q, pivot, pivots)
            if q == step - 1:
                break
            factor = jnp.where(small > q, columns[q] / pivot, 0.0)
            panel = panel - factor * panel[q : q + 1, :]
            for s in range(q + 1, step):
                columns[s] = columns[s] - factor * columns[s][q : q + 1, :]
        inv_ref[pl.ds(begin, step), :] = panel[:, width:] / jnp.sqrt(pivots)
        below = jnp.where(lanes >= begin + step, panel[:, :width] / pivots, 0.0)
        work[...] = work[...] - lax.dot_general(
            below, panel, TN, precision=EXACT, preferred_element_type=jnp.float32
        )

    inverse = inv_ref[...]
    half = lax.dot_general(
        inverse, projected_t, NT, precision=EXACT, preferred_element_type=jnp.float32
    )
    ritz_ref[...] = lax.dot_general(
        half, inverse, NT, precision=EXACT, preferred_element_type=jnp.float32
    )
    own = jnp.where(my == 0, inverse[:modes], pltpu.roll(inverse[modes:], modes, 1))
    inv_t[...] = own.astype(jnp.bfloat16)
    for t in range(0, tiles, 2):
        pair = jnp.concatenate(
            [jnp.concatenate([level2[u], other[u]], axis=0) for u in (t, t + 1)], axis=1
        )
        basis_ref[:, t * size : (t + 2) * size] = lax.dot_general(
            inv_t[...], pair, NN, preferred_element_type=jnp.float32
        ).astype(jnp.bfloat16)
    for c in range(chunks):
        exchange(c).wait_send()


def shards(parts, stiffness_tiles, tile_cols, send_rows, block, lower_bound, upper_bound):
    row_count, modes = block.shape
    tiles, nnz, size = stiffness_tiles.shape[:3]
    slots = send_rows.shape[1]
    width = 2 * modes
    stages = parts.bit_length() - 1
    assert 1 << stages == parts
    chunks = 4
    smem = pl.BlockSpec(memory_space=pltpu.SMEM)
    vmem = pl.BlockSpec(memory_space=pltpu.VMEM)
    dma = pltpu.SemaphoreType.DMA
    level = pltpu.VMEM((tiles + 2 * slots, modes, size), jnp.bfloat16)
    field = pltpu.VMEM((tiles, modes, size), jnp.bfloat16)
    basis, ritz = pl.pallas_call(
        functools.partial(kernel, parts),
        out_shape=(
            jax.ShapeDtypeStruct((modes, row_count), jnp.bfloat16),
            jax.ShapeDtypeStruct((width, width), jnp.float32),
        ),
        in_specs=[smem, smem, smem, smem, vmem, pl.BlockSpec(memory_space=pl.ANY)],
        out_specs=(vmem, vmem),
        scratch_shapes=[
            pltpu.VMEM(stiffness_tiles.shape, jnp.bfloat16),
            level, level, level, field, field, field,
            pltpu.VMEM((3, 2 * slots, modes, size), jnp.bfloat16),
            pltpu.VMEM((stages + 1, width, width), jnp.float32),
            pltpu.VMEM((stages + 1, width, width), jnp.float32),
            pltpu.VMEM((width, 2 * width), jnp.float32),
            pltpu.VMEM((width, width), jnp.float32),
            pltpu.VMEM((modes, width), jnp.bfloat16),
            dma((4,)), dma((3, 2)), dma((3, 2)), dma((chunks,)), dma((chunks,)),
            dma((stages + 1,)), dma((stages + 1,)),
        ],
        compiler_params=pltpu.CompilerParams(
            collective_id=0, has_side_effects=True, vmem_limit_bytes=60 * 1024 * 1024
        ),
    )(tile_cols.T, send_rows, lower_bound, upper_bound, block.T, stiffness_tiles)
    return basis.T, ritz


def solution(mesh):
    placed = (
        P("dof", None, None, None),
        P("dof", None),
        P("dof", None),
        P("dof", "mode"),
        P(),
        P(),
    )
    return jax.shard_map(
        functools.partial(shards, mesh.shape["dof"]),
        mesh=mesh, in_specs=placed, out_specs=(P("dof", "mode"), P()), check_vma=False,
    )
```

time: 248 us -> 60 us (0.24)
  waiting for transfers between devices: 96.8 us -> 0 us
  Pallas kernels: 0 us -> 54.5 us
  local copies, waits for them, and re-layouts: 45.2 us -> 3.34 us
  matrix products: 36.1 us -> 0 us
  other arithmetic: 25.1 us -> 0 us
  starting transfers between devices: 18 us -> 0 us
  between operations: 15.7 us -> 1.93 us
  blocking collectives: 9.84 us -> 0 us
    psum x1 -> x0, waiting for transfers between devices: 91.5 us -> none  [shards(): gram_cols, proj_cols = lax.psum((gram_part, proj_part), 'dof')]
    pallas_call x0 -> x1, Pallas kernels: none -> 54.5 us  [shards(): pl.pallas_call(functools.partial(kernel, parts), out_shape=(jax.ShapeDtyp...]
    gather x9 -> x0, local copies, waits for them, and re-layouts: 43.4 us -> none  [the longest x3 40 us: apply_stiffness(): picked = extended[tile_cols]]
    dot_general x8 -> x0, matrix products: 35.8 us -> none  [the longest x3 27.7 us: apply_stiffness(): jnp.einsum('rkij,rkjm->rim', stiffness_tiles, picked, preferred_element_t...]
    another operation x5 -> x0, other arithmetic: 22.9 us -> none  [the longest x3 12.4 us: reduce_factor(): factor = jnp.linalg.cholesky(gram_matrix)]
    ppermute x6 -> x0, starting transfers between devices: 17.7 us -> none  [shifted(): return lax.ppermute(block, axis, route)]
    all_gather x2 -> x0, blocking collectives: 9.84 us -> none  [the longest x1 5.04 us: shards(): lax.all_gather(gram_cols, 'mode', axis=1, tiled=True)]
    ppermute x6 -> x0, waiting for transfers between devices: 5.19 us -> none  [shifted(): return lax.ppermute(block, axis, route)]
  transfers between devices with their start and end apart: 8 -> 0, of which waited for: 4 -> 0; matrix products, arithmetic and copies ran while one was open for 10% -> 0% of each run, Pallas kernels for 0% -> 0%
where the time goes in v1:
time: 60 us; the launch traced here: 59.7 us
  Pallas kernels  54.5 us (91%)
  local copies, waits for them, and re-layouts  3.34 us (6%)
  between operations  1.93 us (3%)
    pallas_call x1, Pallas kernels, shards(): pl.pallas_call(functools.partial(kernel, parts), out_shape=(jax.ShapeDtyp...  54.5 us
    unnamed x2, local copies, waits for them, and re-layouts  3.34 us

profile of v1, /device:TPU:0, one launch (start us, length us, event | category | flops | bytes accessed | tf_op | source)
XLA Modules:
  0.0 59.7 jit_solution(6458448668883974238)
XLA Ops:
  1.9 54.5 %shard_map.77 = (bf16[64,4096]{1,0:T(8,128)(2,1)}, f32[128,128]{1,0:T(8,128)}) custom-call(s32[10,32]{1,0:T(8,128)} %bitcast.5, s32[2,8]{1,0:T(2,128)} %rows.1, f32[1]{0:T(128)S(6)} %copy.10.low_ref, f32[1]{0:T(128)S(6)} %copy.11.high_ref, bf16[64,4096]{1,0:T(8,128)(2,1)} %bitcast.4, bf16[32,10,128,128]{3,2,1,0:T(8,128)(2,1)} %a_hbm.1), custom_call_target="tpu_custom_call" | custom-call | tf_op jit(solution)/shard_map/pallas_call | solution.py:283
  56.4 1.9 %copy.12 = bf16[4096,64]{0,1:T(8,128)(2,1)} copy(bf16[4096,64]{0,1:T(8,128)(2,1)} %bitcast.3) | data formatting | bytes 1048576
  58.2 1.5 %copy.13 = f32[128,128]{1,0:T(8,128)} copy(f32[128,128]{1,0:T(8,128)} %get-tuple-element.9) | data formatting | bytes 131072

commit v2 on v1

--- a/solution.py
+++ b/solution.py
@@ -17,7 +17,7 @@
 def kernel(
     parts, cols, rows, low_ref, high_ref, x_ref, a_hbm, basis_ref, ritz_ref,
     a_ref, level0, level1, level2, plain, image, other, sends, ar_send, ar_recv,
-    work, inv_ref, inv_t,
+    whole, final_send, final_recv, work, inv_ref, inv_t,
     a_sem, halo_send, halo_recv, mode_send, mode_recv, ar_ssem, ar_rsem,
 ):
     tiles, nnz, size = a_ref.shape[0], a_ref.shape[1], a_ref.shape[2]
@@ -192,12 +192,15 @@
         total = lax.fori_loop(0, part_rows // 4, accumulate, total)
     total = jnp.where(my == 1, pltpu.roll(total, modes, 1), total)
 
-    for s in range(stages + 1):
-        partner = (flipped(1 << s), my) if s < stages else (p, 1 - my)
-        ar_send[s] = total
+    core = lax.rem(p, 2)
+    start_own = pl.multiple_of(core * modes, modes)
+    start_out = pl.multiple_of((1 - core) * modes, modes)
+    whole[...] = total
+
+    def transfer(s, source, target, partner):
         copy = pltpu.make_async_remote_copy(
-            src_ref=ar_send.at[s],
-            dst_ref=ar_recv.at[s],
+            src_ref=source,
+            dst_ref=target,
             send_sem=ar_ssem.at[s],
             recv_sem=ar_rsem.at[s],
             device_id=partner,
@@ -205,14 +208,25 @@
         )
         copy.start()
         copy.wait()
+
+    transfer(0, whole.at[pl.ds(start_out, modes)], ar_recv.at[0], (flipped(1), my))
+    part = whole[pl.ds(start_own, modes), :] + ar_recv[0]
+    for s in range(1, stages + 1):
+        partner = (flipped(1 << s), my) if s < stages else (p, 1 - my)
+        ar_send[s] = part
+        transfer(s, ar_send.at[s], ar_recv.at[s], partner)
         if s < stages:
-            total = total + ar_recv[s]
+            part = part + ar_recv[s]
     theirs = ar_recv[stages]
+    low_part = jnp.where(my == 0, part, theirs)
+    high_part = jnp.where(my == 0, theirs, part)
+    final_send[:modes] = low_part
+    final_send[modes:] = high_part
+    transfer(stages + 1, final_send, final_recv, (flipped(1), my))
+    mine, received = final_send[...], final_recv[...]
     count = parts * tiles * size
-    lower = jnp.where(my == 0, total, theirs) / count
-    upper = jnp.where(my == 0, theirs, total) / count
-    gram = jnp.concatenate([lower[:modes], upper[:modes]], axis=0)
-    projected_t = jnp.concatenate([lower[modes:], upper[modes:]], axis=0)
+    gram = jnp.where(core == 0, mine, received) / count
+    projected_t = jnp.where(core == 0, received, mine) / count
 
     step = 16
     row_id = lax.broadcasted_iota(jnp.int32, (width, width), 0)
@@ -292,13 +306,16 @@
             pltpu.VMEM(stiffness_tiles.shape, jnp.bfloat16),
             level, level, level, field, field, field,
             pltpu.VMEM((3, 2 * slots, modes, size), jnp.bfloat16),
-            pltpu.VMEM((stages + 1, width, width), jnp.float32),
-            pltpu.VMEM((stages + 1, width, width), jnp.float32),
+            pltpu.VMEM((stages + 1, modes, width), jnp.float32),
+            pltpu.VMEM((stages + 1, modes, width), jnp.float32),
+            pltpu.VMEM((width, width), jnp.float32),
+            pltpu.VMEM((width, width), jnp.float32),
+            pltpu.VMEM((width, width), jnp.float32),
             pltpu.VMEM((width, 2 * width), jnp.float32),
             pltpu.VMEM((width, width), jnp.float32),
             pltpu.VMEM((modes, width), jnp.bfloat16),
             dma((4,)), dma((3, 2)), dma((3, 2)), dma((chunks,)), dma((chunks,)),
-            dma((stages + 1,)), dma((stages + 1,)),
+            dma((stages + 2,)), dma((stages + 2,)),
         ],
         compiler_params=pltpu.CompilerParams(
             collective_id=0, has_side_effects=True, vmem_limit_bytes=60 * 1024 * 1024

time: 60 us -> 58.9 us (0.982)
  Pallas kernels: 54.5 us -> 53.2 us
    pallas_call x1, Pallas kernels: 54.5 us -> 53.2 us  [shards(): pl.pallas_call(functools.partial(kernel, parts), out_shape=(jax.ShapeDtyp...]
where the time goes in v2:
time: 58.9 us; the launch traced here: 58.5 us
  Pallas kernels  53.2 us (90%)
  local copies, waits for them, and re-layouts  3.34 us (6%)
  between operations  1.93 us (3%)
    pallas_call x1, Pallas kernels, shards(): pl.pallas_call(functools.partial(kernel, parts), out_shape=(jax.ShapeDtyp...  53.2 us
    unnamed x2, local copies, waits for them, and re-layouts  3.34 us

profile of v2, /device:TPU:0, one launch (start us, length us, event | category | flops | bytes accessed | tf_op | source)
XLA Modules:
  0.0 58.5 jit_solution(14102258932626489051)
XLA Ops:
  1.9 53.2 %shard_map.77 = (bf16[64,4096]{1,0:T(8,128)(2,1)}, f32[128,128]{1,0:T(8,128)}) custom-call(s32[10,32]{1,0:T(8,128)} %bitcast.5, s32[2,8]{1,0:T(2,128)} %rows.1, f32[1]{0:T(128)S(6)} %copy.10.low_ref, f32[1]{0:T(128)S(6)} %copy.11.high_ref, bf16[64,4096]{1,0:T(8,128)(2,1)} %bitcast.4, bf16[32,10,128,128]{3,2,1,0:T(8,128)(2,1)} %a_hbm.1), custom_call_target="tpu_custom_call" | custom-call | tf_op jit(solution)/shard_map/pallas_call | solution.py:297
  55.2 1.9 %copy.12 = bf16[4096,64]{0,1:T(8,128)(2,1)} copy(bf16[4096,64]{0,1:T(8,128)(2,1)} %bitcast.3) | data formatting | bytes 1048576
  57.0 1.5 %copy.13 = f32[128,128]{1,0:T(8,128)} copy(f32[128,128]{1,0:T(8,128)} %get-tuple-element.9) | data formatting | bytes 131072
